TPU v7x, 32 devices: a whole 2x2x4 slice. The times are simulated.
32 devices in a mesh: mod: 4 (over y, x), seq: 8 (over z, core).
Axes of the slice: x: 2, y: 2, z: 4, core: 2. Of those that a mesh axis runs over, the one named last changes fastest.
Arguments:
- tokens: bfloat16 [2048, 4096], P(('mod', 'seq')), may hold values from -6 to 6
- norm_gain: float32 [3, 4096], replicated, may hold values from 0.2 to 2.6
- qkv_weight: bfloat16 [3, 4096, 12288], P(None, None, 'seq'), may hold values from -0.45 to 0.45
- out_weight: bfloat16 [3, 4096, 4096], P(None, 'seq'), may hold values from -0.375 to 0.375
- modality: int32 [16], replicated, may hold values from 0 to 2
- doc_lengths: int32 [4], replicated, may hold values from 1 to 1024, 2048 in all
Outputs:
- mixed: bfloat16 [2048, 4096], P(('mod', 'seq'))
Inputs may be any that keep to these rules, and one draw needn't show every extreme that they name: `doc_lengths`: the lengths sum to 2048; documents follow one another from position 0 in the given order.
All inputs are finite; a program needn't handle non-finite values.
Results may differ from a plain program's by a relative error of at most 0.015.
Values may be sent and summed in bfloat16 or wider, within the bound.
A program may use at most 128 MiB of HBM per device.

v0:
```python
import functools
import math

import jax
import jax.numpy as jnp
from jax import lax
from jax.experimental import pallas as pl
from jax.experimental.pallas import tpu as pltpu
from jax.sharding import PartitionSpec as P

HDIM = 128
MESH = pl.DeviceIdType.MESH
F32 = jnp.float32
BF16 = jnp.bfloat16


def mul(x, k):
    return pl.multiple_of(x, k)


def remote(src, dst, send, recv, dev):
    return pltpu.make_async_remote_copy(
        src_ref=src, dst_ref=dst, send_sem=send, recv_sem=recv,
        device_id=dev, device_id_type=MESH,
    )


def greet(devs):
    barrier = pltpu.get_barrier_semaphore()
    for dev in devs:
        pl.semaphore_signal(barrier, inc=1, device_id=dev, device_id_type=MESH)
    pl.semaphore_wait(barrier, len(devs))


def sublayer(
    n, modality, doc_lengths, tokens, gain, w_hbm, o_hbm, out,
    wv, xg, stage, q_out, kv_out, att, pairbuf, bias, right_in, left_in,
    w_sem, o_sem, own_s, fs, fr, ps, pr, a_s, a_r, b_s, b_r, ps2, pr2, rs, rr, ls, lr,
):
    m = lax.axis_index("mod")
    s = lax.axis_index("seq")
    chip, core = s // 2, s % 2
    rows, width = tokens.shape
    pair = 2 * rows
    group = n * pair
    half = n // 2
    feats = q_out.shape[1]
    heads = feats // HDIM
    mods = w_hbm.shape[0]
    right = (m, ((chip + 1) % n) * 2 + core)
    left = (m, ((chip + n - 1) % n) * 2 + core)
    partner = (m, chip * 2 + (1 - core))
    chunks = 2
    piece = rows // chunks

    w_copies = [pltpu.make_async_copy(w_hbm.at[k], wv.at[k], w_sem.at[k]) for k in range(mods)]
    for c in w_copies:
        c.start()

    values = tokens[...].astype(F32)
    inv = lax.rsqrt(jnp.mean(values * values, axis=1, keepdims=True) + 1e-05)
    row_gain = gain[pl.ds(modality[m * n + chip], 1), :]
    xg[pl.ds(mul(chip * pair + core * rows, rows), rows), :] = (values * inv * row_gain).astype(BF16)

    @pl.when(m < 2)
    def _():
        kv_out[pl.ds(0, group), :] = jnp.zeros((group, 2 * feats), BF16)

    @pl.when(m < 1)
    def _():
        kv_out[pl.ds(group, group), :] = jnp.zeros((group, 2 * feats), BF16)

    others = [((m + d) % 4, s) for d in range(1, 4)]
    greet([right, left, partner] + others)

    def ref(block, which, c):
        return xg.at[pl.ds(mul(block * pair + which * rows + c * piece, piece), piece), :]

    def to_partner(block, c):
        r = ref(block, core, c)
        return remote(r, r, ps.at[block, c], pr.at[block, c], partner)

    def from_partner(block, c):
        r = ref(block, 1 - core, c)
        return remote(r, r, ps.at[block, c], pr.at[block, c], partner)

    def onward(block, c, dev, sem):
        r = ref(block, core, c)
        return remote(r, r, sem, fr.at[block, c], dev)

    for c in range(chunks):
        @pl.when(chip < n - 1)
        def _(c=c):
            onward(chip, c, right, own_s.at[0, c]).start()

        @pl.when(chip > 0)
        def _(c=c):
            onward(chip, c, left, own_s.at[1, c]).start()
    for c in range(chunks):
        to_partner(chip, c).start()

    def handle(k, c):
        for sign, dev in ((-1, right), (1, left)):
            block = chip + sign * k
            following = chip - sign

            @pl.when((block >= 0) & (block < n))
            def _(block=block, following=following, dev=dev):
                onward(block, c, dev, fs.at[block, c]).wait_recv()

                @pl.when((following >= 0) & (following < n))
                def _():
                    onward(block, c, dev, fs.at[block, c]).start()

                to_partner(block, c).start()

    def settle():
        for c in range(chunks):
            @pl.when(chip < n - 1)
            def _(c=c):
                onward(chip, c, right, own_s.at[0, c]).wait_send()

            @pl.when(chip > 0)
            def _(c=c):
                onward(chip, c, left, own_s.at[1, c]).wait_send()

            for d in range(n):
                to_partner((chip + d) % n, c).wait_send()
            for k in range(1, n):
                for sign, dev in ((-1, right), (1, left)):
                    block = chip + sign * k
                    following = chip - sign

                    @pl.when((block >= 0) & (block < n) & (following >= 0) & (following < n))
                    def _(block=block, dev=dev, c=c):
                        onward(block, c, dev, fs.at[block, c]).wait_send()

    tile = 256 if (3 * feats) % 256 == 0 else 128
    upper = chip // half
    near_side = chip * (1 - upper) + (n - 1 - chip) * upper
    far_sign = 1 - 2 * upper

    def block_at(t):
        if t == 0:
            return chip
        step = (t + 1) // 2
        two = step if t % 2 == 0 else -step
        past = (t - 1 - 2 * near_side + 2 * n) // (2 * n)
        return chip + two * (1 - past) + far_sign * (t - near_side) * past

    def own_copies(t, r):
        pieces = 4 if t == n - 1 else 1
        size = pair // pieces

        def copies(seg_from, seg_to, send, recv, to):
            return [
                remote(
                    kv_out.at[pl.ds(mul(seg_from * group + r + p * size, size), size), :],
                    kv_out.at[pl.ds(mul(seg_to * group + r + p * size, size), size), :],
                    send.at[t + p], recv.at[t + p], (to, s),
                )
                for p in range(pieces)
            ]

        return {
            "near01": copies(2, 1, a_s, a_r, 1),
            "far02": copies(2, 0, b_s, b_r, 2),
            "far13": copies(2, 0, b_s, b_r, 3),
            "near23": copies(2, 1, a_s, a_r, 3),
            "near32": copies(0, 1, a_s, a_r, 2),
        }

    own_sends = (("near01", "far02"), ("far13",), ("near23",), ("near32",))
    arrivals = ((), ("near01",), ("near32", "far02"), ("near23",))

    plan = []
    forwarded = []

    def forward_to(count):
        for t in range(len(forwarded), count):
            forwarded.append(t)

            @pl.when(m == 3)
            def _(t=t):
                for came, goes in zip(plan[t]["far13"], plan[t]["near32"]):
                    came.wait_recv()
                    goes.start()

    def project():
        t = len(plan)
        block = block_at(t)
        r = mul(block * pair, pair)
        mode = modality[m * n + block]
        for c in range(chunks):
            from_partner(block, c).wait_recv()

        def one_tile(j, carry):
            cols = pl.ds(mul(j * tile, tile), tile)
            stage[:, cols] = jnp.dot(
                xg[pl.ds(r, pair), :], wv[mode, :, cols], preferred_element_type=F32
            ).astype(BF16)
            return carry

        lax.fori_loop(0, 3 * feats // tile, one_tile, 0)
        for h in range(heads):
            q_out[pl.ds(r, pair), pl.ds(h * HDIM, HDIM)] = stage[:, pl.ds(3 * h * HDIM, HDIM)]
            kv_out[pl.ds(mul(2 * group + r, pair), pair), pl.ds(2 * h * HDIM, 2 * HDIM)] = stage[
                :, pl.ds((3 * h + 1) * HDIM, 2 * HDIM)
            ]
        copies = own_copies(t, r)
        plan.append(copies)
        for who in range(3):
            @pl.when(m == who)
            def _(who=who):
                for name in own_sends[who]:
                    for c in copies[name]:
                        c.start()
        forward_to(t)

    for c in range(chunks - 1):
        handle(1, c)
    for c in w_copies:
        c.wait()
    project()
    handle(1, chunks - 1)
    project()
    for k in range(2, n):
        for c in range(chunks):
            handle(k, c)
        project()
    squares = width // feats
    o_copies = [
        pltpu.make_async_copy(
            o_hbm.at[k, :, pl.ds(c * feats, feats)],
            wv.at[k, pl.ds(c * feats, feats), pl.ds(0, feats)],
            o_sem.at[k * squares + c],
        )
        for c in range(squares) for k in range(mods)
    ]
    for c in o_copies:
        c.start()
    forward_to(n)
    settle()
    for who in range(4):
        @pl.when(m == who)
        def _(who=who):
            for copies in plan:
                for name in arrivals[who]:
                    for c in copies[name]:
                        c.wait_recv()

    q, kv = q_out, kv_out
    keys = 3 * group
    chunk = keys
    while chunk > 1536:
        chunk //= 2
    scale = math.log2(math.e) / math.sqrt(HDIM)
    first_key = (m - 2) * group
    def mine(t):
        return pl.ds(mul(t * pair + core * rows, rows), rows)

    def theirs(t):
        return pl.ds(mul(t * pair + (1 - core) * rows, rows), rows)

    waited = []

    def compute(t, off):
        r = mul(((chip + off + n) % n) * pair, pair)
        pos = m * group + r + lax.broadcasted_iota(jnp.int32, (pair, 1), 0)
        end = jnp.int32(0)
        start = jnp.zeros((pair, 1), jnp.int32)
        for d in range(doc_lengths.shape[0]):
            end = end + doc_lengths[d]
            start = jnp.where(pos >= end, end, start)
        for c0 in range(0, keys, chunk):
            key = first_key + c0 + lax.broadcasted_iota(jnp.int32, (pair, chunk), 1)
            bias[:, pl.ds(c0, chunk)] = jnp.where((key <= pos) & (key >= start), 0.0, -1e30)
        for h in range(heads):
            query = q[pl.ds(r, pair), pl.ds(h * HDIM, HDIM)]
            top = total = acc = None
            for c0 in reversed(range(0, keys, chunk)):
                k_part = kv[pl.ds(c0, chunk), pl.ds(2 * h * HDIM, HDIM)]
                v_part = kv[pl.ds(c0, chunk), pl.ds((2 * h + 1) * HDIM, HDIM)]
                scores = lax.dot_general(
                    query, k_part, (((1,), (1,)), ((), ())), preferred_element_type=F32
                ) * scale + bias[:, pl.ds(c0, chunk)]
                peak = jnp.max(scores, axis=1, keepdims=True)
                new_top = peak if top is None else jnp.maximum(top, peak)
                weights = jnp.exp2(scores - new_top)
                if chunk != keys:
                    weights = jnp.where(bias[:, pl.ds(c0, chunk)] < 0.0, 0.0, weights)
                row_sum = jnp.sum(weights, axis=1, keepdims=True)
                added = jnp.dot(weights.astype(BF16), v_part, preferred_element_type=F32)
                if top is None:
                    total, acc = row_sum, added
                else:
                    fix = jnp.exp2(top - new_top)
                    total, acc = total * fix + row_sum, acc * fix + added
                top = new_top
            att[:, pl.ds(h * HDIM, HDIM)] = (acc / total).astype(BF16)
        if not waited:
            for c in o_copies:
                c.wait()
            waited.append(True)
        mode = modality[m * n + (chip + off + n) % n]

        def one_tile(j, carry):
            cols = pl.ds(mul(j * feats, feats), feats)
            square = wv[mode, cols, pl.ds(0, feats)]
            xg[pl.ds(t * pair, pair), cols] = jnp.dot(
                att[...], square, preferred_element_type=F32
            ).astype(BF16)
            return carry

        lax.fori_loop(0, squares, one_tile, 0)
        copy = remote(xg.at[theirs(t), :], pairbuf.at[t], ps2.at[t], pr2.at[t], partner)
        copy.start()
        return copy

    lo, hi = pl.ds(0, width // 2), pl.ds(width // 2, width // 2)
    sent = []

    def pair_sum(t, copy):
        copy.wait_recv()
        sent.append(copy)
        return xg[mine(t), :].astype(F32) + pairbuf[t].astype(F32)

    def send(src, dst, ss, rsm, dev):
        copy = remote(src, dst, ss, rsm, dev)
        copy.start()
        sent.append(copy)
        return copy

    copy = compute(0, half)
    xg[mine(0), :] = pair_sum(0, copy).astype(BF16)
    r_prev = send(xg.at[mine(0), lo], right_in.at[half - 1, :, lo], rs.at[half - 1], rr.at[half - 1], right)
    l_prev = send(xg.at[mine(0), hi], left_in.at[half - 1, :, hi], ls.at[half - 1], lr.at[half - 1], left)
    t = 1
    for k in range(half - 1, 0, -1):
        c_right = compute(t, k)
        c_left = compute(t + 1, -k)
        for which, (tt, c, prev, inbox, ss, rsm, dev, cols) in enumerate((
            (t, c_right, r_prev, right_in, rs, rr, right, lo),
            (t + 1, c_left, l_prev, left_in, ls, lr, left, hi),
        )):
            total = pair_sum(tt, c)
            prev.wait_recv()
            if k == half - 1:
                a, b = total[:, : width // 2], total[:, width // 2:]
                if which == 0:
                    a = a + inbox[k, :, lo].astype(F32)
                else:
                    b = b + inbox[k, :, hi].astype(F32)
                xg[mine(tt), lo] = a.astype(BF16)
                xg[mine(tt), hi] = b.astype(BF16)
            else:
                xg[mine(tt), :] = (total + inbox[k].astype(F32)).astype(BF16)
            new = send(xg.at[mine(tt), :], inbox.at[k - 1], ss.at[k - 1], rsm.at[k - 1], dev)
            if which == 0:
                r_prev = new
            else:
                l_prev = new
        t += 2
    c = compute(t, 0)
    total = pair_sum(t, c) + tokens[...].astype(F32)
    r_prev.wait_recv()
    total = total + right_in[0].astype(F32)
    l_prev.wait_recv()
    out[...] = (total + left_in[0].astype(F32)).astype(BF16)
    for copy in sent:
        copy.wait_send()


    for who in range(4):
        @pl.when(m == who)
        def _(who=who):
            for copies in plan:
                for name in own_sends[who]:
                    for c in copies[name]:
                        c.wait_send()


def body(n, tokens, norm_gain, qkv_weight, out_weight, modality, doc_lengths):
    rows, width = tokens.shape
    feats = out_weight.shape[1]
    mods = out_weight.shape[0]
    pair = 2 * rows
    group = n * pair
    half = n // 2
    vmem = pl.BlockSpec(memory_space=pltpu.VMEM)
    smem = pl.BlockSpec(memory_space=pltpu.SMEM)
    hbm = pl.BlockSpec(memory_space=pl.ANY)
    dma = pltpu.SemaphoreType.DMA
    limit = 62 * 1024 * 1024
    return pl.pallas_call(
        functools.partial(sublayer, n),
        out_shape=jax.ShapeDtypeStruct((rows, width), BF16),
        in_specs=[smem, smem, vmem, vmem, hbm, hbm],
        out_specs=vmem,
        scratch_shapes=[
            pltpu.VMEM((mods, width, 3 * feats), BF16),
            pltpu.VMEM((group, width), BF16),
            pltpu.VMEM((pair, 3 * feats), BF16),
            pltpu.VMEM((group, feats), BF16),
            pltpu.VMEM((3 * group, 2 * feats), BF16),
            pltpu.VMEM((pair, feats), BF16),
            pltpu.VMEM((n, rows, width), BF16),
            pltpu.VMEM((pair, 3 * group), F32),
            pltpu.VMEM((half, rows, width), BF16),
            pltpu.VMEM((half, rows, width), BF16),
            dma((mods,)), dma((mods * (width // feats),)),
            dma((2, 2)), dma((n, 2)), dma((n, 2)), dma((n, 2)), dma((n, 2)),
            dma((n + 3,)), dma((n + 3,)), dma((n + 3,)), dma((n + 3,)),
            dma((n,)), dma((n,)),
            dma((half,)), dma((half,)), dma((half,)), dma((half,)),
        ],
        compiler_params=pltpu.CompilerParams(
            collective_id=0, has_side_effects=True, vmem_limit_bytes=limit
        ),
    )(modality, doc_lengths, tokens, norm_gain, qkv_weight, out_weight)


def solution(mesh):
    return jax.shard_map(
        functools.partial(body, mesh.shape["seq"] // 2),
        mesh=mesh,
        in_specs=(
            P(("mod", "seq"), None),
            P(),
            P(None, None, "seq"),
            P(None, "seq", None),
            P(),
            P(),
        ),
        out_specs=P(("mod", "seq"), None),
        check_vma=False,
    )
```

profile of v0, /device:TPU:12, one launch (start us, length us, event | category | flops | bytes accessed | tf_op | source)
XLA Modules:
  0.0 100.9 jit_solution(12074562585508852951)
XLA Ops:
  0.0 99.0 %shard_map.64 = bf16[64,4096]{1,0:T(8,128)(2,1)} custom-call(s32[16]{0:T(128)} %modality.1, s32[4]{0:T(128)} %doc_lengths.1, bf16[64,4096]{1,0:T(8,128)(2,1)} %tokens.1, f32[3,4096]{1,0:T(4,128)} %gain.1, bf16[3,4096,1536]{2,1,0:T(8,128)(2,1)} %w_hbm.1, bf16[3,512,4096]{2,1,0:T(8,128)(2,1)} %o_hbm.1), custom_call_target="tpu_custom_call" | custom-call | tf_op jit(solution)/shard_map/pallas_call | solution.py:395
  99.0 1.9 %copy.8 = bf16[64,4096]{1,0:T(8,128)(2,1)} copy(bf16[64,4096]{1,0:T(8,128)(2,1)} %shard_map.64) | data formatting | bytes 1048576
where the time goes:
time: 101 us
  Pallas kernels  99 us (98%)
  local copies, waits for them, and re-layouts  1.87 us (2%)
    pallas_call x1, Pallas kernels, body(): pl.pallas_call(functools.partial(sublayer, n), out_shape=jax.ShapeDtypeSt...  99 us

commit v1 on v0

--- a/solution.py
+++ b/solution.py
@@ -12,6 +12,10 @@
 MESH = pl.DeviceIdType.MESH
 F32 = jnp.float32
 BF16 = jnp.bfloat16
+LINES = 4
+PIECES = 4
+HALVES = 2
+TILES = 2
 
 
 def mul(x, k):
@@ -420,9 +424,511 @@
     )(modality, doc_lengths, tokens, norm_gain, qkv_weight, out_weight)
 
 
+def phased(
+    n, modality, doc_lengths, tokens, gain, w_hbm, o_hbm, out,
+    wq, wo, xg, stage, qkv, ao, ai, pb, rin, fin,
+    w_sem, ys, other_s, fa, ne, po, fs, fr, ps, pr, qs, qr, as_, ar, bs, br, rs, rr, es, er,
+):
+    m = lax.axis_index("mod")
+    s = lax.axis_index("seq")
+    chip, core = s // 2, s % 2
+    upper, parity = m // 2, m % 2
+    across = (m + 2) % LINES
+    rows, width = tokens.shape
+    half = rows // 2
+    pair = 2 * rows
+    group = n * pair
+    total_rows = LINES * group
+    mods, feats, _ = o_hbm.shape
+    share = qkv.shape[1]
+    heads = share // (3 * HDIM)
+    right = (m, ((chip + 1) % n) * 2 + core)
+    left = (m, ((chip + n - 1) % n) * 2 + core)
+    partner = (m, chip * 2 + (1 - core))
+    hold = core == upper
+
+    w_copies = [pltpu.make_async_copy(w_hbm.at[k], wq.at[k], w_sem.at[k]) for k in range(mods)]
+    o_copies = [pltpu.make_async_copy(o_hbm.at[k], wo.at[k], w_sem.at[mods]) for k in range(mods)]
+    for c in w_copies + o_copies:
+        c.start()
+    o_done = pltpu.make_async_copy(o_hbm, wo, w_sem.at[mods])
+
+    barrier = pltpu.get_barrier_semaphore()
+    known = [partner, (across, chip * 2 + (1 - core))]
+    known += [((m + d) % LINES, s) for d in range(1, LINES)]
+    for dev in known:
+        pl.semaphore_signal(barrier, inc=1, device_id=dev, device_id_type=MESH)
+
+    @pl.when(chip < n - 1)
+    def _():
+        pl.semaphore_signal(barrier, inc=1, device_id=right, device_id_type=MESH)
+
+    @pl.when(chip > 0)
+    def _():
+        pl.semaphore_signal(barrier, inc=1, device_id=left, device_id_type=MESH)
+
+    values = tokens[...].astype(F32)
+    inv = lax.rsqrt(jnp.mean(values * values, axis=1, keepdims=True) + 1e-05)
+    row_gain = gain[pl.ds(modality[m * n + chip], 1), :]
+    normed = (values * inv * row_gain).astype(BF16)
+
+    @pl.when(hold)
+    def _():
+        xg[upper, chip] = normed
+
+    @pl.when(jnp.logical_not(hold))
+    def _():
+        out[...] = normed
+
+    pl.semaphore_wait(barrier, len(known) + jnp.minimum(chip, 1) + jnp.minimum(n - 1 - chip, 1))
+
+    def send(copy, cond=None):
+        if cond is None:
+            copy.start()
+        else:
+            pl.when(cond)(copy.start)
+
+    def settled(ref, sem, cond=None):
+        copy = remote(ref, ref, sem, fr.at[0, 0, 0], partner)
+        if cond is None:
+            copy.wait_send()
+        else:
+            pl.when(cond)(copy.wait_send)
+
+    def arrive(copy, cond=None):
+        if cond is None:
+            copy.wait_recv()
+        else:
+            pl.when(cond)(copy.wait_recv)
+
+    def strip(c):
+        return pl.ds(c * (width // PIECES), width // PIECES)
+
+    def part(k, block, which, c):
+        return xg.at[k, block, pl.ds(mul(which * half, half), half), strip(c)]
+
+    def along(k, block, c, dev, sem):
+        r = part(k, block, core, c)
+        return remote(r, r, sem, fr.at[k, block, c], dev)
+
+    def to_partner(k, block, c, sem):
+        r = part(k, block, core, c)
+        return remote(r, r, sem, pr.at[k, block], partner)
+
+    def from_partner(k, block):
+        r = xg.at[k, block, pl.ds(mul((1 - core) * half, half), half), :]
+        return remote(r, r, ps.at[k], pr.at[k, block], partner)
+
+    moved = [
+        remote(
+            out.at[pl.ds(r * half, half), strip(c)], part(upper, chip, r, c),
+            ys.at[0], fr.at[upper, chip, c], (across, chip * 2 + r),
+        )
+        for c in range(PIECES) for r in range(2)
+    ]
+    for copy in moved:
+        pl.when(jnp.logical_not(hold))(copy.start)
+
+    middle = n // 2
+    beyond = chip // middle
+    near_side = chip * (1 - beyond) + (n - 1 - chip) * beyond
+    far_sign = 1 - 2 * beyond
+
+    for c in range(PIECES):
+        r = part(upper, chip, 1 - core, c)
+        send(remote(r, r, other_s.at[0], fr.at[upper, chip, c], partner), hold)
+
+    def unit_source(k):
+        return (upper == k) & hold
+
+    def enter_far(k, when, pieces=range(PIECES), both=False):
+        source = unit_source(k)
+        for c in pieces:
+            arrive(along(k, chip, c, right, fa.at[k]), when & jnp.logical_not(source))
+            send(along(k, chip, c, right, fa.at[k]), when & (beyond == 0))
+            send(along(k, chip, c, left, fa.at[k]), when & (beyond == 1))
+            if both:
+                enter_near(k, when, (c,))
+            send(to_partner(k, chip, c, po.at[k]), when & (source | (upper != k)))
+
+    def enter_near(k, when, pieces=range(PIECES)):
+        inner = when & (near_side > 0)
+        for c in pieces:
+            send(along(k, chip, c, left, ne.at[k]), inner & (beyond == 0))
+            send(along(k, chip, c, right, ne.at[k]), inner & (beyond == 1))
+
+    def handle(k, j, c, who=None):
+        for sign, dev in ((-1, right), (1, left)):
+            block = chip + sign * j
+            following = chip - sign
+            there = (block >= 0) & (block < n)
+            if who is not None:
+                there = there & (near_side > 0 if who == "inner" else near_side == 0)
+            goes = there & (following >= 0) & (following < n)
+            copy = along(k, block, c, dev, fs.at[k])
+            arrive(copy, there)
+            send(copy, goes)
+            send(to_partner(k, block, c, ps.at[k]), there)
+
+    def settle(k):
+        unit = xg.at[k, 0, pl.ds(0, half), :]
+        rest = xg.at[k, pl.ds(0, n - 1), pl.ds(0, half), :]
+        inner = near_side > 0
+        settled(unit, fa.at[k])
+        settled(unit, ne.at[k], inner)
+        settled(unit, po.at[k], unit_source(k) | (upper != k))
+        settled(unit, other_s.at[0], hold & (upper == k))
+        settled(rest, fs.at[k], inner)
+        settled(rest, ps.at[k])
+
+    def block_at(t):
+        if t == 0:
+            return chip
+        step = (t + 1) // 2
+        two = far_sign * (step if t % 2 == 1 else -step)
+        past = (t - 1 - 2 * near_side + 2 * n) // (2 * n)
+        return chip + two * (1 - past) + far_sign * (t - near_side) * past
+
+    def order(t):
+        return block_at(n - 1 - t)
+
+    def place(line, k, block):
+        at = ((2 * k + line % 2) * n + block) * pair + (line // 2) * rows
+        return pl.ds(mul(at, rows), rows)
+
+    def mode_of(k, block):
+        return modality[(2 * k + parity) * n + block]
+
+    def give(k, t, block, to):
+        return remote(
+            stage.at[t, to], qkv.at[place(m, k, block), :], qs.at[k, t], qr.at[k], (to, s)
+        )
+
+    def project(k, t, hold_back=False):
+        block = block_at(t)
+        if t > 0:
+            from_partner(k, block).wait_recv()
+        else:
+            pl.when(jnp.logical_not(unit_source(k)))(from_partner(k, block).wait_recv)
+        if k == 1:
+            settled(stage.at[t, pl.ds(0, LINES - 1)], qs.at[0, t])
+        mode = mode_of(k, block)
+        per = LINES // TILES
+        tile = per * share
+
+        def one_tile(i, carry):
+            j = (i + 1 + m // per) % TILES
+            cols = pl.ds(mul(j * tile, 128), tile)
+            got = jnp.dot(xg[k, block], wq[mode, :, cols], preferred_element_type=F32).astype(BF16)
+            for i in range(per):
+                to = j * per + i
+                stage[t, to] = got[:, i * share:(i + 1) * share]
+                if not hold_back:
+                    pl.when(to != m)(give(k, t, block, to).start)
+            return carry
+
+        lax.fori_loop(0, TILES, one_tile, 0)
+        qkv[place(m, k, block), :] = stage[t, m]
+
+    def give_back(k, t):
+        for off in range(1, LINES):
+            give(k, t, block_at(t), (m + off) % LINES).start()
+
+    def gathered(k):
+        r = qkv.at[pl.ds(0, n * (LINES - 1) * rows), :]
+        remote(r, r, qs.at[k, 0], qr.at[k], partner).wait_recv()
+
+    scale = math.log2(math.e) / math.sqrt(HDIM)
+    look = total_rows // 2
+
+    def attend(k, t):
+        block = order(t)
+        for a in range(2):
+            q0 = mul(((2 * k + a) * n + block) * pair, pair)
+            if k == 0:
+                k0, span = 0, (a + 1) * group
+            else:
+                k0, span = mul(q0 - look, pair), look + pair
+            pos = q0 + lax.broadcasted_iota(jnp.int32, (pair, 1), 0)
+            end = jnp.int32(0)
+            start = jnp.zeros((pair, 1), jnp.int32)
+            for d in range(doc_lengths.shape[0]):
+                end = end + doc_lengths[d]
+                start = jnp.where(pos >= end, end, start)
+            key = k0 + lax.broadcasted_iota(jnp.int32, (pair, span), 1)
+            allowed = (key <= pos) & (key >= start)
+            for h in range(heads):
+                base = 3 * h * HDIM
+                query = qkv[pl.ds(q0, pair), pl.ds(base, HDIM)]
+                keys = qkv[pl.ds(k0, span), pl.ds(base + HDIM, HDIM)]
+                vals = qkv[pl.ds(k0, span), pl.ds(base + 2 * HDIM, HDIM)]
+                scores = lax.dot_general(
+                    query, keys, (((1,), (1,)), ((), ())), preferred_element_type=F32
+                ) * scale
+                scores = jnp.where(allowed, scores, -1e30)
+                weights = jnp.exp2(scores - jnp.max(scores, axis=1, keepdims=True))
+                row_sum = jnp.sum(weights, axis=1, keepdims=True)
+                acc = jnp.dot(weights.astype(BF16), vals, preferred_element_type=F32)
+                ao[pl.ds(q0, pair), pl.ds(h * HDIM, HDIM)] = (acc / row_sum).astype(BF16)
+        for off in range(1, LINES):
+            to = (m + off) % LINES
+            send(remote(ao.at[place(to, k, block), :], ai.at[k, t, m], as_.at[k], ar.at[k, t], (to, s)))
+        ai[k, t, m] = ao[place(m, k, block), :]
+
+    def emit(k, t):
+        block = order(t)
+        r = ai.at[k, t, pl.ds(0, LINES - 1)]
+        remote(r, r, as_.at[k], ar.at[k, t], partner).wait_recv()
+        mode = mode_of(k, block)
+        att = jnp.concatenate([ai[k, t, i] for i in range(LINES)], axis=1)
+        tile = width // HALVES
+        for j in range(HALVES):
+            cols = pl.ds(j * tile, tile)
+            xg[k, block, :, cols] = jnp.dot(att, wo[mode, :, cols], preferred_element_type=F32).astype(BF16)
+            send(pair_copy(k, t, j))
+
+    def pair_copy(k, t, c):
+        cols = pl.ds(c * (width // HALVES), width // HALVES)
+        r = xg.at[k, order(t), pl.ds(mul((1 - core) * half, half), half), cols]
+        return remote(r, pb.at[k, t, :, cols], bs.at[k], br.at[k, t, c], partner)
+
+    own_rows = pl.ds(mul(core * half, half), half)
+
+    def inbox(k, slot, c):
+        return rin.at[k, slot, :, strip(c)]
+
+    def take(k, slot, c):
+        r = inbox(k, slot, c)
+        remote(r, r, rs.at[k], rr.at[k, slot, c], partner).wait_recv()
+
+    def onward(k, block, c, rightward, leftward):
+        r = xg.at[k, block, own_rows, strip(c)]
+        send(
+            remote(r, inbox(k, block, c), rs.at[k], rr.at[k, block, c], right),
+            rightward,
+        )
+        slot = block + (n - block) * (1 - jnp.minimum(jnp.abs(chip - 1 - block), 1))
+        send(
+            remote(r, inbox(k, slot, c), rs.at[k], rr.at[k, slot, c], left),
+            leftward,
+        )
+
+    def pair_wait(k, t, c):
+        each = PIECES // HALVES
+        if c % each == 0:
+            pair_copy(k, t, c // each).wait_recv()
+
+    def begin(k, t, c):
+        block = order(t)
+
+        @pl.when(near_side == 0)
+        def _():
+            pair_wait(k, t, c)
+            xg[k, block, own_rows, strip(c)] = (
+                xg[k, block, own_rows, strip(c)].astype(F32) + pb[k, t, :, strip(c)].astype(F32)
+            ).astype(BF16)
+
+        onward(k, block, c, chip == 0, chip == n - 1)
+
+    def carry(k, t):
+        block = order(t)
+        inner = near_side > 0
+        for c in range(PIECES):
+            @pl.when(inner)
+            def _():
+                pair_wait(k, t, c)
+                take(k, block, c)
+                xg[k, block, own_rows, strip(c)] = (
+                    xg[k, block, own_rows, strip(c)].astype(F32) + pb[k, t, :, strip(c)].astype(F32)
+                    + rin[k, block, :, strip(c)].astype(F32)
+                ).astype(BF16)
+
+            onward(k, block, c, inner & (block > chip), inner & (block < chip))
+
+    def finish(k):
+        t = n - 1
+        here = (upper == k) & hold
+        away = jnp.logical_not(here)
+        to = m + (across - m) * jnp.abs(upper - k)
+        for c in range(PIECES):
+            pair_wait(k, t, c)
+            pl.when(chip > 0)(functools.partial(take, k, chip, c))
+            pl.when(chip < n - 1)(functools.partial(take, k, n, c))
+            total = xg[k, chip, own_rows, strip(c)].astype(F32) + pb[k, t, :, strip(c)].astype(F32)
+            low = jnp.where(chip > 0, rin[k, chip, :, strip(c)].astype(F32), 0.0)
+            high = jnp.where(chip < n - 1, rin[k, n, :, strip(c)].astype(F32), 0.0)
+            total = total + low + high
+
+            @pl.when(here)
+            def _():
+                out[own_rows, strip(c)] = (tokens[own_rows, strip(c)].astype(F32) + total).astype(BF16)
+
+            @pl.when(away)
+            def _():
+                xg[k, chip, own_rows, strip(c)] = total.astype(BF16)
+
+            send(
+                remote(
+                    xg.at[k, chip, own_rows, strip(c)], fin.at[own_rows, strip(c)],
+                    es.at[k], er.at[core, c], (to, chip * 2 + upper),
+                ), away,
+            )
+
+    def last(which, c):
+        at = pl.ds(mul(which * half, half), half)
+        r = fin.at[at, strip(c)]
+        remote(r, r, es.at[0], er.at[which, c], partner).wait_recv()
+        out[at, strip(c)] = (tokens[at, strip(c)].astype(F32) + fin[at, strip(c)].astype(F32)).astype(BF16)
+
+    def many(k, j, who=None, part_of=range(PIECES)):
+        for c in part_of:
+            handle(k, j, c, who)
+
+    def start(k, t):
+        for c in range(PIECES):
+            begin(k, t, c)
+
+    first, second = range(PIECES // 2), range(PIECES // 2, PIECES)
+
+    enter_far(1, upper == 1, first, both=True)
+    enter_far(0, upper >= 0, both=True)
+    many(0, 1)
+    enter_far(1, upper == 0, first)
+    enter_far(1, upper >= 0, second)
+    for c in w_copies:
+        c.wait()
+    many(0, 2, "inner", first)
+    project(0, 0)
+    many(0, 2, "inner", second)
+    enter_near(1, upper == 0, first)
+    enter_near(1, upper >= 0, second)
+    many(0, 2, "edge", first)
+    project(0, 1)
+    many(0, 2, "edge", second)
+    many(1, 1, "inner")
+    for t in range(2, n - 1):
+        if t > 2:
+            many(0, t)
+        project(0, t)
+    many(1, 2, "inner", first)
+    many(0, n - 1)
+    project(0, n - 1)
+    many(1, 2, "inner", second)
+    project(1, 0)
+    o_done.wait()
+    pl.when(jnp.logical_not(hold))(lambda: settled(out, ys.at[0]))
+    settle(0)
+    gathered(0)
+    attend(0, 0)
+    attend(0, 1)
+    many(1, 1, "edge")
+    project(1, 1, hold_back=True)
+    many(1, 2, "edge")
+    emit(0, 0)
+    attend(0, 2)
+    start(0, 0)
+    emit(0, 1)
+    for t in range(3, n):
+        attend(0, t)
+    give_back(1, 1)
+    for u in range(2, n):
+        if u + 1 < n:
+            many(1, u + 1)
+        project(1, u)
+        if u == 2:
+            start(0, 1)
+    for t in range(2, n):
+        emit(0, t)
+        if t > 2:
+            start(0, t - 1)
+    settle(1)
+    carry(0, 0)
+    gathered(1)
+    for t in range(n - 1):
+        attend(1, t)
+        if t > 0 and t < n - 2:
+            carry(0, t)
+    emit(1, 0)
+    attend(1, n - 1)
+    start(1, 0)
+    carry(0, n - 2)
+    emit(1, 1)
+    for t in range(2, n):
+        emit(1, t)
+        start(1, t - 1)
+    finish(0)
+    for t in range(n - 1):
+        carry(1, t)
+    finish(1)
+
+    @pl.when(hold)
+    def _():
+        for c in range(PIECES):
+            last(1 - core, c)
+
+    @pl.when(jnp.logical_not(hold))
+    def _():
+        for c in range(PIECES):
+            for which in range(2):
+                last(which, c)
+    for k in range(2):
+        if k == 1:
+            for t in range(n):
+                settled(stage.at[t, pl.ds(0, LINES - 1)], qs.at[k, t])
+        back = ao.at[pl.ds(0, n * (LINES - 1) * rows), :]
+        settled(back, as_.at[k])
+        settled(pb.at[k], bs.at[k])
+        settled(rin.at[k, pl.ds(0, n - 1)], rs.at[k])
+        settled(xg.at[k, 0, pl.ds(0, half), :], es.at[k], jnp.logical_not(unit_source(k)))
+
+
+def phased_body(n, tokens, norm_gain, qkv_weight, out_weight, modality, doc_lengths):
+    rows, width = tokens.shape
+    mods, feats, _ = out_weight.shape
+    pair = 2 * rows
+    share = 3 * feats // LINES
+    vmem = pl.BlockSpec(memory_space=pltpu.VMEM)
+    smem = pl.BlockSpec(memory_space=pltpu.SMEM)
+    hbm = pl.BlockSpec(memory_space=pl.ANY)
+    dma = pltpu.SemaphoreType.DMA
+    return pl.pallas_call(
+        functools.partial(phased, n),
+        out_shape=jax.ShapeDtypeStruct((rows, width), BF16),
+        in_specs=[smem, smem, vmem, vmem, hbm, hbm],
+        out_specs=vmem,
+        scratch_shapes=[
+            pltpu.VMEM((mods, width, 3 * feats), BF16),
+            pltpu.VMEM((mods, feats, width), BF16),
+            pltpu.VMEM((2, n, rows, width), BF16),
+            pltpu.VMEM((n, LINES, rows, share), BF16),
+            pltpu.VMEM((LINES * n * pair, share), BF16),
+            pltpu.VMEM((LINES * n * pair, share // 3), BF16),
+            pltpu.VMEM((2, n, LINES, rows, share // 3), BF16),
+            pltpu.VMEM((2, n, rows // 2, width), BF16),
+            pltpu.VMEM((2, n + 1, rows // 2, width), BF16),
+            pltpu.VMEM((rows, width), BF16),
+            dma((mods + 1,)), dma((1,)), dma((1,)), dma((2,)), dma((2,)), dma((2,)),
+            dma((2,)), dma((2, n, PIECES)), dma((2,)), dma((2, n)),
+            dma((2, n)), dma((2,)), dma((2,)), dma((2, n)),
+            dma((2,)), dma((2, n, HALVES)), dma((2,)), dma((2, n + 1, PIECES)),
+            dma((2,)), dma((2, PIECES)),
+        ],
+        compiler_params=pltpu.CompilerParams(
+            collective_id=0, has_side_effects=True, vmem_limit_bytes=67043328
+        ),
+    )(modality, doc_lengths, tokens, norm_gain, qkv_weight, out_weight)
+
+
+def either(n, lines, tokens, norm_gain, qkv_weight, out_weight, modality, doc_lengths):
+    heads = out_weight.shape[1] // HDIM
+    fits = lines == LINES and heads % LINES == 0 and n % 2 == 0
+    run = phased_body if fits else body
+    return run(n, tokens, norm_gain, qkv_weight, out_weight, modality, doc_lengths)
+
+
 def solution(mesh):
     return jax.shard_map(
-        functools.partial(body, mesh.shape["seq"] // 2),
+        functools.partial(either, mesh.shape["seq"] // 2, mesh.shape["mod"]),
         mesh=mesh,
         in_specs=(
             P(("mod", "seq"), None),

time: 101 us -> 85.6 us (0.85)
  Pallas kernels: 99 us -> 83.6 us
    pallas_call x1, Pallas kernels: 99 us -> 83.6 us  [phased_body(): pl.pallas_call(functools.partial(phased, n), out_shape=jax.ShapeDtypeStru...]
where the time goes in v1:
time: 85.6 us; the launch traced here: 85.5 us
  Pallas kernels  83.6 us (98%)
  local copies, waits for them, and re-layouts  1.87 us (2%)
    pallas_call x1, Pallas kernels, phased_body(): pl.pallas_call(functools.partial(phased, n), out_shape=jax.ShapeDtypeStru...  83.6 us
    unnamed x1, local copies, waits for them, and re-layouts  1.87 us

profile of v1, /device:TPU:12, one launch (start us, length us, event | category | flops | bytes accessed | tf_op | source)
XLA Modules:
  0.0 85.5 jit_solution(4793627470707594979)
XLA Ops:
  0.0 83.6 %shard_map.64 = bf16[64,4096]{1,0:T(8,128)(2,1)} custom-call(s32[16]{0:T(128)} %modality.1, s32[4]{0:T(128)} %doc_lengths.1, bf16[64,4096]{1,0:T(8,128)(2,1)} %tokens.1, f32[3,4096]{1,0:T(4,128)} %gain.1, bf16[3,4096,1536]{2,1,0:T(8,128)(2,1)} %w_hbm.1, bf16[3,512,4096]{2,1,0:T(8,128)(2,1)} %o_hbm.1), custom_call_target="tpu_custom_call" | custom-call | tf_op jit(solution)/shard_map/pallas_call | solution.py:894
  83.6 1.9 %copy.8 = bf16[64,4096]{1,0:T(8,128)(2,1)} copy(bf16[64,4096]{1,0:T(8,128)(2,1)} %shard_map.64) | data formatting | bytes 1048576

commit v2 on v1

--- a/solution.py
+++ b/solution.py
@@ -730,20 +730,22 @@
 
         onward(k, block, c, chip == 0, chip == n - 1)
 
-    def carry(k, t):
-        block = order(t)
+    def carry(k, *steps):
         inner = near_side > 0
         for c in range(PIECES):
-            @pl.when(inner)
-            def _():
-                pair_wait(k, t, c)
-                take(k, block, c)
-                xg[k, block, own_rows, strip(c)] = (
-                    xg[k, block, own_rows, strip(c)].astype(F32) + pb[k, t, :, strip(c)].astype(F32)
-                    + rin[k, block, :, strip(c)].astype(F32)
-                ).astype(BF16)
-
-            onward(k, block, c, inner & (block > chip), inner & (block < chip))
+            for t in steps:
+                block = order(t)
+
+                @pl.when(inner)
+                def _():
+                    pair_wait(k, t, c)
+                    take(k, block, c)
+                    xg[k, block, own_rows, strip(c)] = (
+                        xg[k, block, own_rows, strip(c)].astype(F32) + pb[k, t, :, strip(c)].astype(F32)
+                        + rin[k, block, :, strip(c)].astype(F32)
+                    ).astype(BF16)
+
+                onward(k, block, c, inner & (block > chip), inner & (block < chip))
 
     def finish(k):
         t = n - 1
@@ -818,47 +820,45 @@
     o_done.wait()
     pl.when(jnp.logical_not(hold))(lambda: settled(out, ys.at[0]))
     settle(0)
+    many(1, 1, "edge")
     gathered(0)
     attend(0, 0)
     attend(0, 1)
-    many(1, 1, "edge")
     project(1, 1, hold_back=True)
     many(1, 2, "edge")
     emit(0, 0)
     attend(0, 2)
     start(0, 0)
+    give_back(1, 1)
+    for u in range(2, n - 1):
+        project(1, u)
+        many(1, u + 1)
     emit(0, 1)
+    project(1, n - 1)
+    start(0, 1)
     for t in range(3, n):
         attend(0, t)
-    give_back(1, 1)
-    for u in range(2, n):
-        if u + 1 < n:
-            many(1, u + 1)
-        project(1, u)
-        if u == 2:
-            start(0, 1)
-    for t in range(2, n):
+    for t in range(2, n - 1):
         emit(0, t)
-        if t > 2:
-            start(0, t - 1)
     settle(1)
+    for t in range(2, n - 1):
+        start(0, t)
     carry(0, 0)
     gathered(1)
     for t in range(n - 1):
         attend(1, t)
-        if t > 0 and t < n - 2:
-            carry(0, t)
+    emit(0, n - 1)
+    carry(0, *range(1, n - 1))
     emit(1, 0)
     attend(1, n - 1)
     start(1, 0)
-    carry(0, n - 2)
     emit(1, 1)
     for t in range(2, n):
         emit(1, t)
         start(1, t - 1)
+    carry(1, 0)
     finish(0)
-    for t in range(n - 1):
-        carry(1, t)
+    carry(1, *range(1, n - 1))
     finish(1)
 
     @pl.when(hold)

time: 85.6 us -> 81.7 us (0.954)
  Pallas kernels: 83.6 us -> 79.6 us
    pallas_call x1, Pallas kernels: 83.6 us -> 79.6 us  [phased_body(): pl.pallas_call(functools.partial(phased, n), out_shape=jax.ShapeDtypeStru...]
where the time goes in v2:
time: 81.7 us; the launch traced here: 81.5 us
  Pallas kernels  79.6 us (97%)
  local copies, waits for them, and re-layouts  1.87 us (2%)
    pallas_call x1, Pallas kernels, phased_body(): pl.pallas_call(functools.partial(phased, n), out_shape=jax.ShapeDtypeStru...  79.6 us
    unnamed x1, local copies, waits for them, and re-layouts  1.87 us

profile of v2, /device:TPU:12, one launch (start us, length us, event | category | flops | bytes accessed | tf_op | source)
XLA Modules:
  0.0 81.5 jit_solution(10042873958297293339)
XLA Ops:
  0.0 79.6 %shard_map.64 = bf16[64,4096]{1,0:T(8,128)(2,1)} custom-call(s32[16]{0:T(128)} %modality.1, s32[4]{0:T(128)} %doc_lengths.1, bf16[64,4096]{1,0:T(8,128)(2,1)} %tokens.1, f32[3,4096]{1,0:T(4,128)} %gain.1, bf16[3,4096,1536]{2,1,0:T(8,128)(2,1)} %w_hbm.1, bf16[3,512,4096]{2,1,0:T(8,128)(2,1)} %o_hbm.1), custom_call_target="tpu_custom_call" | custom-call | tf_op jit(solution)/shard_map/pallas_call | solution.py:894
  79.6 1.9 %copy.8 = bf16[64,4096]{1,0:T(8,128)(2,1)} copy(bf16[64,4096]{1,0:T(8,128)(2,1)} %shard_map.64) | data formatting | bytes 1048576

commit v3 on v2

--- a/solution.py
+++ b/solution.py
@@ -816,7 +816,7 @@
     many(0, n - 1)
     project(0, n - 1)
     many(1, 2, "inner", second)
-    project(1, 0)
+    project(1, 0, hold_back=True)
     o_done.wait()
     pl.when(jnp.logical_not(hold))(lambda: settled(out, ys.at[0]))
     settle(0)
@@ -824,18 +824,20 @@
     gathered(0)
     attend(0, 0)
     attend(0, 1)
+    give_back(1, 0)
     project(1, 1, hold_back=True)
     many(1, 2, "edge")
     emit(0, 0)
     attend(0, 2)
     start(0, 0)
     give_back(1, 1)
+    emit(0, 1)
     for u in range(2, n - 1):
+        many(1, u + 1)
         project(1, u)
-        many(1, u + 1)
-    emit(0, 1)
+        if u == 2:
+            start(0, 1)
     project(1, n - 1)
-    start(0, 1)
     for t in range(3, n):
         attend(0, t)
     for t in range(2, n - 1):

time: 81.7 us -> 81.3 us (level)
  no operation moved by 1% of the time
where the time goes in v3:
time: 81.3 us; the launch traced here: 81.1 us
  Pallas kernels  79.2 us (97%)
  local copies, waits for them, and re-layouts  1.87 us (2%)
    pallas_call x1, Pallas kernels, phased_body(): pl.pallas_call(functools.partial(phased, n), out_shape=jax.ShapeDtypeStru...  79.2 us
    unnamed x1, local copies, waits for them, and re-layouts  1.87 us

profile of v3, /device:TPU:12, one launch (start us, length us, event | category | flops | bytes accessed | tf_op | source)
XLA Modules:
  0.0 81.1 jit_solution(16697295485489919214)
XLA Ops:
  0.0 79.2 %shard_map.64 = bf16[64,4096]{1,0:T(8,128)(2,1)} custom-call(s32[16]{0:T(128)} %modality.1, s32[4]{0:T(128)} %doc_lengths.1, bf16[64,4096]{1,0:T(8,128)(2,1)} %tokens.1, f32[3,4096]{1,0:T(4,128)} %gain.1, bf16[3,4096,1536]{2,1,0:T(8,128)(2,1)} %w_hbm.1, bf16[3,512,4096]{2,1,0:T(8,128)(2,1)} %o_hbm.1), custom_call_target="tpu_custom_call" | custom-call | tf_op jit(solution)/shard_map/pallas_call | solution.py:896
  79.2 1.9 %copy.8 = bf16[64,4096]{1,0:T(8,128)(2,1)} copy(bf16[64,4096]{1,0:T(8,128)(2,1)} %shard_map.64) | data formatting | bytes 1048576
